TPU v7x, 32 devices: a whole 2x2x4 slice. The times are simulated.
32 devices in a mesh: dp: 16 (over z, y, core), level: 2 (over x).
Axes of the slice: x: 2, y: 2, z: 4, core: 2. Of those that a mesh axis runs over, the one named last changes fastest.
Arguments:
- token_ids: int32 [16, 2, 1536], P('dp', 'level'), may hold values from 0 to 1023
- decoded_mask: int32 [16, 2, 1536], P('dp', 'level'), may hold values 0 or 1
- levels_done: int32 [16], P('dp'), may hold values from 0 to 1
- code_tables: bfloat16 [2, 1024, 1024], P('level'), may hold values from -6 to 6
- mask_vectors: bfloat16 [2, 1024], P('level'), may hold values from -6 to 6
- w_qkv: bfloat16 [3, 1024, 1024], P(None, 'dp', 'level'), may hold values from -6 to 6
- w_out: bfloat16 [1024, 1024], P('level', 'dp'), may hold values from -0.1875 to 0.1875
- w_expand: bfloat16 [1024, 2048], P('dp'), may hold values from -0.1875 to 0.1875
- w_depth: bfloat16 [5, 1024], replicated, may hold values from -2.5 to 2.5
- w_project: bfloat16 [1024, 1024], P('dp'), may hold values from -0.1875 to 0.1875
- level_heads: bfloat16 [2, 1024, 1024], P('level'), may hold values from -0.1875 to 0.1875
Outputs:
- logits: bfloat16 [16, 2, 1536, 1024], P('dp', 'level')
Inputs may be any that keep to these rules, and one draw needn't show every extreme that they name: `levels_done`: levels below it are fully decoded; the level equal to it is the one being decoded.
All inputs are finite; a program needn't handle non-finite values. No bound on the sum of `decoded_mask` on one device may be relied on, other than what follows from the above.
Results may differ from a plain program's by a relative error of at most 0.006.
Values may be sent and summed in bfloat16 or wider, within the bound.
A program may use at most 192 MiB of HBM per device.

v0:
```python
import functools
import math

import jax
import jax.numpy as jnp
from jax import lax
from jax.experimental import pallas as pl
from jax.experimental.pallas import tpu as pltpu
from jax.sharding import PartitionSpec as P

HEADS = 16
CORES = 2
LANES = 128
HALO = 16
MESH = pl.DeviceIdType.MESH


def layer_norm(values):
    centered = values - jnp.mean(values, axis=-1, keepdims=True)
    variance = jnp.mean(centered * centered, axis=-1, keepdims=True)
    return centered * lax.rsqrt(variance + 1e-05)


def dot_f32(left, right):
    return jnp.dot(left, right, preferred_element_type=jnp.float32)


def dot_nt(left, right):
    return lax.dot_general(left, right, (((1,), (1,)), ((), ())), preferred_element_type=jnp.float32)


def chip_at(position, chips):
    position = lax.rem(position + 2 * chips, chips)
    turned = position // (chips // 2)
    return (1 - turned) * 2 * position + turned * (2 * (chips - 1 - position) + 1)


def position_of(chip, chips):
    odd = lax.rem(chip, 2)
    return (1 - odd) * (chip // 2) + odd * (chips - 1 - chip // 2)


class Ring:
    def __init__(self, full, rows, chips, sems):
        self.full, self.rows, self.chips, self.half = full, rows, chips, chips // 2
        self.send, self.recv, self.sib_send, self.sib_recv = sems
        self.device = lax.axis_index("dp")
        self.core = lax.rem(self.device, CORES)
        self.position = position_of(self.device // CORES, chips)
        self.sent = []

    def block(self, position, core, part):
        row = (chip_at(position, self.chips) * CORES + core) * self.rows
        count = self.rows
        if part is not None:
            count = self.rows // 2
            row = row + part * count
        return self.full.at[:, pl.ds(pl.multiple_of(row, count), count), :]

    def part(self, way, step):
        return way if step == self.half - 1 else None

    def origin(self, way, step):
        return self.position - (1 + step) if way == 0 else self.position + (1 + step)

    def hop(self, way, step):
        towards = self.position + 1 if way == 0 else self.position - 1
        source = self.position - step if way == 0 else self.position + step
        ref = self.block(source, self.core, self.part(way, step))
        target = chip_at(towards, self.chips) * CORES + self.core
        return pltpu.make_async_remote_copy(
            src_ref=ref,
            dst_ref=ref,
            send_sem=self.send.at[way, step],
            recv_sem=self.recv.at[way, step],
            device_id={"dp": target},
            device_id_type=MESH,
        )

    def arrival(self, way, step):
        ref = self.block(self.origin(way, step), self.core, self.part(way, step))
        return pltpu.make_async_remote_copy(
            src_ref=ref,
            dst_ref=ref,
            send_sem=self.send.at[way, step],
            recv_sem=self.recv.at[way, step],
            device_id={"dp": self.device},
            device_id_type=MESH,
        )

    def share(self, way, step, core):
        position = self.position if step < 0 else self.origin(way, step)
        ref = self.block(position, core, None if step < 0 else self.part(way, step))
        sibling = self.device + 1 - 2 * self.core
        return pltpu.make_async_remote_copy(
            src_ref=ref,
            dst_ref=ref,
            send_sem=self.sib_send.at[way, step + 1],
            recv_sem=self.sib_recv.at[way, step + 1],
            device_id={"dp": sibling},
            device_id_type=MESH,
        )

    def start(self):
        for way in range(2):
            self.hop(way, 0).start()
        self.share(0, -1, self.core).start()

    def advance(self, step):
        for way in range(2):
            self.arrival(way, step).wait_recv()
            if step + 1 < self.half:
                self.hop(way, step + 1).start()
            self.share(way, step, self.core).start()

    def finish(self):
        for way in range(2):
            for step in range(self.half):
                self.hop(way, step).wait_send()
                self.share(way, step, self.core).wait_send()
                self.share(way, step, 1 - self.core).wait_recv()
        self.share(0, -1, self.core).wait_send()
        self.share(0, -1, 1 - self.core).wait_recv()


def step_kernel(
    levels, devices, frames, width,
    meta_ref, table_ref, qkv_ref, out_ref, expand_ref, project_ref, head_ref, depth_ref,
    logits_ref,
    metas, tables, proj, rest_ref, embedded, normed, keys, values, queries,
    attended, gated, final, head,
    halo_send, halo_recv, final_send, final_recv,
    local_sem, level_send, level_recv, table_send, table_recv,
    ring_a, ring_a_recv, sib_a, sib_a_recv, ring_b, ring_b_recv, sib_b, sib_b_recv,
):
    level = lax.axis_index("level")
    device = lax.axis_index("dp")
    core = lax.rem(device, CORES)
    sibling = device + 1 - 2 * core
    chips = devices // CORES
    rows = width // devices
    columns = width // levels
    local_rows = frames // levels
    codes = table_ref.shape[0]
    half_table = codes // CORES
    position = position_of(device // CORES, chips)

    barrier = pltpu.get_barrier_semaphore()
    for shift in range(1, levels):
        pl.semaphore_signal(barrier, inc=1, device_id={"level": lax.rem(level + shift, levels)}, device_id_type=MESH)
    for other in (
        sibling,
        chip_at(position + 1, chips) * CORES + core,
        chip_at(position - 1, chips) * CORES + core,
    ):
        pl.semaphore_signal(barrier, inc=1, device_id={"dp": other}, device_id_type=MESH)
    pl.semaphore_wait(barrier, levels + 2)

    own_rows = pl.ds(pl.multiple_of(device * rows, rows), rows)
    own_columns = pl.ds(pl.multiple_of(level * columns, columns), columns)
    places = (
        (qkv_ref, proj.at[:, own_rows, own_columns]),
        (out_ref, rest_ref.at[pl.ds(0, 1), own_rows, own_columns]),
        (meta_ref, metas.at[level]),
    )
    half_rows = pl.ds(pl.multiple_of(core * half_table, half_table), half_table)
    other_half = pl.ds(pl.multiple_of((1 - core) * half_table, half_table), half_table)

    def over_level(kind, shift):
        source, place = places[kind]
        return pltpu.make_async_remote_copy(
            src_ref=source, dst_ref=place,
            send_sem=level_send.at[kind, shift], recv_sem=level_recv.at[kind, shift],
            device_id={"level": lax.rem(level + shift, levels)}, device_id_type=MESH,
        )

    def from_level(kind, shift):
        sender = lax.rem(level + levels - shift, levels)
        sender_columns = pl.ds(pl.multiple_of(sender * columns, columns), columns)
        source = places[kind][0]
        place = (
            proj.at[:, own_rows, sender_columns],
            rest_ref.at[pl.ds(0, 1), own_rows, sender_columns],
            metas.at[sender],
        )[kind]
        return pltpu.make_async_remote_copy(
            src_ref=source, dst_ref=place,
            send_sem=level_send.at[kind, shift], recv_sem=level_recv.at[kind, shift],
            device_id={"level": sender}, device_id_type=MESH,
        )

    def table_out(shift):
        return pltpu.make_async_remote_copy(
            src_ref=table_ref.at[half_rows], dst_ref=tables.at[level, half_rows],
            send_sem=table_send.at[0, shift], recv_sem=table_recv.at[0, shift],
            device_id={"level": lax.rem(level + shift, levels)}, device_id_type=MESH,
        )

    def table_at(shift, span, kind):
        sender = lax.rem(level + levels - shift, levels)
        place = tables.at[sender, span]
        return pltpu.make_async_remote_copy(
            src_ref=place, dst_ref=place,
            send_sem=table_send.at[kind, shift], recv_sem=table_recv.at[kind, shift],
            device_id={"dp": sibling}, device_id_type=MESH,
        )

    locals_ = [
        pltpu.make_async_copy(source, place, local_sem.at[i]) for i, (source, place) in enumerate(places)
    ] + [
        pltpu.make_async_copy(table_ref, tables.at[level], local_sem.at[3]),
        pltpu.make_async_copy(expand_ref.at[:, pl.ds(0, width)], rest_ref.at[1, own_rows, :], local_sem.at[4]),
        pltpu.make_async_copy(expand_ref.at[:, pl.ds(width, width)], rest_ref.at[2, own_rows, :], local_sem.at[5]),
        pltpu.make_async_copy(project_ref, rest_ref.at[3, own_rows, :], local_sem.at[6]),
    ]
    head_copy = pltpu.make_async_copy(head_ref, head, local_sem.at[7])
    for kind in (0, 2):
        for shift in range(1, levels):
            over_level(kind, shift).start()
    for copy in locals_:
        copy.start()
    for shift in range(1, levels):
        table_out(shift).start()
    for shift in range(1, levels):
        over_level(1, shift).start()
    head_copy.start()

    def rings(full, count, sems):
        return [
            Ring(full.at[pl.ds(piece, 1)], rows, chips, tuple(sem.at[piece] for sem in sems))
            for piece in range(count)
        ]

    first = rings(proj, 3, (ring_a, ring_a_recv, sib_a, sib_a_recv))
    second = rings(rest_ref, 4, (ring_b, ring_b_recv, sib_b, sib_b_recv))

    for copy in locals_:
        copy.wait()
    for shift in range(1, levels):
        from_level(0, shift).wait_recv()
    hops = chips // 2
    for ring in first:
        ring.start()
    for step in range(hops - 1):
        for ring in first:
            ring.advance(step)
    for shift in range(1, levels):
        from_level(1, shift).wait_recv()
    for ring in second:
        ring.start()
    for shift in range(1, levels):
        from_level(2, shift).wait_recv()
        table_at(shift, half_rows, 0).wait_recv()
        table_at(shift, half_rows, 1).start()
    for shift in range(1, levels):
        table_at(shift, half_rows, 1).wait_send()
        table_at(shift, other_half, 1).wait_recv()

    tile = 2 * LANES
    @pl.loop(0, frames // tile)
    def _(step):
        for piece, ring in enumerate(first):
            @pl.when(step == min(2 + piece, frames // tile - 1))
            def _():
                ring.advance(hops - 1)

        span = pl.ds(pl.multiple_of(step * tile, tile), tile)
        total = jnp.zeros((tile, width), jnp.float32)
        lane = lax.broadcasted_iota(jnp.int32, (tile, LANES), 1).astype(jnp.float32)
        for row in range(levels):
            ids = jnp.concatenate(
                [
                    jnp.broadcast_to(
                        metas[row, 0:1, pl.ds(pl.multiple_of(step * tile + piece * LANES, LANES), LANES)],
                        (LANES, LANES),
                    ).T
                    for piece in range(tile // LANES)
                ],
                axis=0,
            )
            onehot = jnp.concatenate(
                [
                    jnp.where(ids == lane + float(base), 1.0, 0.0).astype(jnp.bfloat16)
                    for base in range(0, codes, LANES)
                ],
                axis=1,
            )
            picked = dot_f32(onehot, tables[row])
            fill = metas[row, 8:9, 0:width]
            total = total + jnp.where(ids[:, 0:1] < 0.0, fill, picked)
        embedded[span, :] = total
        normed[span, :] = layer_norm(total).astype(jnp.bfloat16)

    for ring in first:
        ring.finish()

    @pl.loop(0, frames // tile)
    def _(step):
        for piece, ring in enumerate(second):
            @pl.when(step == min(2 + piece, frames // tile - 1))
            def _():
                ring.advance(0)

        span = pl.ds(pl.multiple_of(step * tile, tile), tile)
        keys[span, :] = dot_f32(normed[span, :], proj[1]).astype(jnp.bfloat16)
        values[span, :] = dot_f32(normed[span, :], proj[2]).astype(jnp.bfloat16)

    head_dim = width // HEADS
    scale = head_dim ** (-0.5)
    block = math.gcd(local_rows, tile)

    @pl.loop(0, local_rows // block)
    def _(step):
        begin = pl.multiple_of(level * local_rows + step * block, block)
        to = pl.ds(pl.multiple_of(step * block, block), block)
        found = dot_f32(normed[pl.ds(begin, block), :], proj[0]).astype(jnp.bfloat16)
        queries[to, :] = found * jnp.asarray(scale, jnp.bfloat16)

    blocks = local_rows // block
    pairs = width // LANES
    turns = pairs * min(2, blocks)
    events = [(step, ring) for step in range(1, hops) for ring in second]
    pad = HALO
    taps = depth_ref.shape[0]
    odd_level = lax.rem(level, 2)

    def chunk_of(owner, order):
        odd = lax.rem(owner, 2)
        return odd * order + (1 - odd) * (blocks - 1 - order)

    def local_span(order):
        return pl.ds(pl.multiple_of(chunk_of(level, order) * block, block), block)

    def clip_span(owner, order):
        start = owner * local_rows + chunk_of(owner, order) * block
        return pl.ds(pl.multiple_of(start, block), block)

    def halo(way):
        source = (pl.ds(local_rows, pad), pl.ds(pad, pad))[way]
        place = (pl.ds(0, pad), pl.ds(pad + local_rows, pad))[way]
        target = level + 1 if way == 0 else level - 1
        return pltpu.make_async_remote_copy(
            src_ref=gated.at[source], dst_ref=gated.at[place],
            send_sem=halo_send.at[way], recv_sem=halo_recv.at[way],
            device_id={"level": target}, device_id_type=MESH,
        )

    has = (level < levels - 1, level > 0)

    def halo_start(way):
        pl.when(has[way])(lambda: halo(way).start())

    def halo_wait(way):
        pl.when(has[1 - way])(lambda: halo(way).wait_recv())

    def spread(owner, order, shift, target):
        return pltpu.make_async_remote_copy(
            src_ref=final.at[clip_span(owner, order)], dst_ref=final.at[clip_span(owner, order)],
            send_sem=final_send.at[order, shift], recv_sem=final_recv.at[order, shift],
            device_id={"level": target}, device_id_type=MESH,
        )

    @pl.when(level == 0)
    def _():
        gated[pl.ds(0, pad), :] = jnp.zeros((pad, width), jnp.bfloat16)

    @pl.when(level == levels - 1)
    def _():
        gated[pl.ds(pad + local_rows, pad), :] = jnp.zeros((pad, width), jnp.bfloat16)

    def attend(order):
        to = local_span(order)

        @pl.loop(0, pairs)
        def _(pair):
            turn = order * pairs + pair
            for event, (step, ring) in enumerate(events):
                @pl.when(turn == event * turns // len(events))
                def _():
                    ring.advance(step)

            across = pl.ds(pl.multiple_of(pair * LANES, LANES), LANES)
            query = queries[to, across]
            key = keys[:, across]
            value = values[:, across]
            lower = lax.broadcasted_iota(jnp.int32, (block, LANES), 1) < head_dim
            lower_value = lax.broadcasted_iota(jnp.int32, (frames, LANES), 1) < head_dim
            one = jnp.ones_like(value)
            zero = jnp.zeros_like(query)
            sums = []
            for low in (True, False):
                masked = jnp.where(lower, query, zero) if low else jnp.where(lower, zero, query)
                scores = dot_nt(masked, key)
                weights = jnp.exp(scores - jnp.max(scores, axis=-1, keepdims=True)).astype(jnp.bfloat16)
                extended = jnp.where(lower_value, value, one) if low else jnp.where(lower_value, one, value)
                sums.append(dot_f32(weights, extended))
            above = jnp.where(lower, sums[0], sums[1])
            below = pltpu.roll(jnp.where(lower, sums[1], sums[0]), head_dim, 1)
            attended[to, across] = (above / below).astype(jnp.bfloat16)

    def gate(order):
        own = clip_span(level, order)
        after_attn = embedded[own, :] + dot_nt(attended[local_span(order), :], rest_ref[0])
        embedded[own, :] = after_attn
        normed_two = layer_norm(after_attn).astype(jnp.bfloat16)
        mixed = dot_f32(normed_two, rest_ref[1]) * jax.nn.sigmoid(dot_f32(normed_two, rest_ref[2]))
        start = pl.multiple_of(pad + chunk_of(level, order) * block, pad)
        gated[pl.ds(start, block), :] = mixed.astype(jnp.bfloat16)

    def convolve(order):
        own = clip_span(level, order)
        start = pl.multiple_of(chunk_of(level, order) * block, block)
        window = gated[pl.ds(start, block + 2 * pad), :].astype(jnp.float32)
        conv = jnp.zeros((block, width), jnp.float32)
        for tap in range(taps):
            first_row = pad - taps // 2 + tap
            conv = conv + window[first_row : first_row + block] * depth_ref[tap : tap + 1, :]
        activated = (conv * jax.nn.sigmoid(conv)).astype(jnp.bfloat16)
        after_conv = embedded[own, :] + dot_f32(activated, rest_ref[3])
        final[own, :] = layer_norm(after_conv).astype(jnp.bfloat16)

    def score(owner, order):
        span = clip_span(owner, order)
        logits_ref[span, :] = dot_f32(final[span, :], head[...]).astype(jnp.bfloat16)

    def send_and_score(order):
        convolve(order)
        for shift in range(1, levels):
            spread(level, order, shift, lax.rem(level + shift, levels)).start()
        score(level, order)

    def by_parity(act, even_way):
        pl.when(odd_level == 0)(lambda: act(even_way))
        pl.when(odd_level == 1)(lambda: act(1 - even_way))

    @pl.loop(0, blocks)
    def _(stage):
        attend(stage)

        @pl.when(stage == 1)
        def _():
            for ring in second:
                ring.finish()
            head_copy.wait()
            gate(0)
            by_parity(halo_start, 0)

        @pl.when(stage >= 1)
        def _():
            gate(stage)

        @pl.when(stage == blocks - 1)
        def _():
            by_parity(halo_start, 1)

        @pl.when(stage == 1)
        def _():
            by_parity(halo_wait, 1)

        @pl.when(stage >= 1)
        def _():
            send_and_score(stage - 1)

    by_parity(halo_wait, 0)
    send_and_score(blocks - 1)

    @pl.loop(0, blocks)
    def _(order):
        for shift in range(1, levels):
            sender = lax.rem(level + levels - shift, levels)
            spread(sender, order, shift, sender).wait_recv()
            score(sender, order)

    for way in range(2):
        pl.when(has[way])(lambda: halo(way).wait_send())
    for shift in range(1, levels):
        table_out(shift).wait_send()
        for kind in range(3):
            over_level(kind, shift).wait_send()

    @pl.loop(0, blocks)
    def _(order):
        for shift in range(1, levels):
            spread(level, order, shift, lax.rem(level + shift, levels)).wait_send()


def decode_step(levels, devices, ids, fill, table, w_qkv, w_out_t, w_expand, w_project, head, taps):
    frames, width = ids.shape[0], table.shape[1]
    chips = devices // CORES
    local_rows = frames // levels
    blocks = local_rows // math.gcd(local_rows, 2 * LANES)
    span = max(frames, width)
    meta = jnp.concatenate(
        [
            jnp.broadcast_to(jnp.pad(ids, (0, span - frames)), (8, span)),
            jnp.broadcast_to(jnp.pad(fill, (0, span - width)), (8, span)),
        ]
    )
    vmem = pl.BlockSpec(memory_space=pltpu.VMEM)
    anywhere = pl.BlockSpec(memory_space=pl.ANY)
    dma = pltpu.SemaphoreType.DMA
    half = chips // 2
    bf16, f32 = jnp.bfloat16, jnp.float32
    return pl.pallas_call(
        functools.partial(step_kernel, levels, devices, frames, width),
        out_shape=jax.ShapeDtypeStruct((frames, head.shape[1]), bf16),
        in_specs=[anywhere] * 7 + [vmem],
        out_specs=vmem,
        scratch_shapes=[
            pltpu.VMEM((levels,) + meta.shape, f32),
            pltpu.VMEM((levels,) + table.shape, bf16),
            pltpu.VMEM((3, width, width), bf16),
            pltpu.VMEM((4, width, width), bf16),
            pltpu.VMEM((frames, width), f32),
            pltpu.VMEM((frames, width), bf16),
            pltpu.VMEM((frames, width), bf16),
            pltpu.VMEM((frames, width), bf16),
            pltpu.VMEM((local_rows, width), bf16),
            pltpu.VMEM((local_rows, width), bf16),
            pltpu.VMEM((local_rows + 2 * HALO, width), bf16),
            pltpu.VMEM((frames, width), bf16),
            pltpu.VMEM(head.shape, bf16),
            dma((2,)), dma((2,)), dma((blocks, levels)), dma((blocks, levels)),
            dma((8,)),
            dma((3, levels)), dma((3, levels)), dma((2, levels)), dma((2, levels)),
        ]
        + [
            dma((count, 2, half + extra)) for count in (3, 4) for extra in (0, 0, 1, 1)
        ],
        compiler_params=pltpu.CompilerParams(
            collective_id=0, has_side_effects=True, vmem_limit_bytes=64000 * 1024
        ),
    )(meta, table, w_qkv, w_out_t, w_expand, w_project, head, taps)


def body(
    token_ids,
    decoded_mask,
    levels_done,
    code_tables,
    mask_vectors,
    w_qkv,
    w_out,
    w_expand,
    w_depth,
    w_project,
    level_heads,
):
    groups = lax.axis_size("level")
    level_index = lax.axis_index("level")
    done_count = levels_done[0]
    use_token = (level_index < done_count) | ((level_index == done_count) & (decoded_mask[0, 0] == 1))
    ids = jnp.where(use_token, token_ids[0, 0], -1).astype(jnp.float32)
    logits = decode_step(
        groups, lax.axis_size("dp"), ids, mask_vectors[0].astype(jnp.float32), code_tables[0],
        w_qkv, w_out.T[None], w_expand, w_project, level_heads[0], w_depth.astype(jnp.float32),
    )
    return logits[None, None]


def solution(mesh):
    return jax.shard_map(
        body,
        mesh=mesh,
        in_specs=(
            P("dp", "level", None),
            P("dp", "level", None),
            P("dp"),
            P("level", None, None),
            P("level", None),
            P(None, "dp", "level"),
            P("level", "dp"),
            P("dp", None),
            P(),
            P("dp", None),
            P("level", None, None),
        ),
        out_specs=P("dp", "level", None, None),
        check_vma=False,
    )
```

profile of v0, /device:TPU:0, one launch (start us, length us, event | category | flops | bytes accessed | tf_op | source)
XLA Modules:
  0.0 154.6 jit_solution(2064952931749076688)
XLA Ops:
  0.7 0.7 reduce.1
  1.4 0.7 convert_reduce_fusion
  2.1 1.3 convert_element_type.14.depth_ref
  3.5 0.6 pad_maximum_fusion.meta_ref
  4.1 146.6 %shard_map.109 = bf16[1536,1024]{1,0:T(8,128)(2,1)} custom-call(f32[16,1536]{1,0:T(8,128)} %pad_maximum_fusion.meta_ref, bf16[1024,1024]{1,0:T(8,128)(2,1)} %bitcast.10, bf16[3,64,512]{2,1,0:T(8,128)(2,1)} %qkv_ref.1, bf16[1,64,512]{2,1,0:T(8,128)(2,1)} %bitcast.12, bf16[64,2048]{1,0:T(8,128)(2,1)} %expand_ref.1, bf16[64,1024]{1,0:T(8,128)(2,1)} %project_ref.1, ...), custom_call_target="tpu_custom_call" | custom-call | tf_op jit(solution)/shard_map/pallas_call | solution.py:504
  150.7 3.9 %copy.14 = bf16[1,1,1536,1024]{3,2,1,0:T(8,128)(2,1)} copy(bf16[1,1,1536,1024]{3,2,1,0:T(8,128)(2,1)} %bitcast.9) | data formatting | bytes 6291456
  (3 shorter events, 0.0 us)
where the time goes:
time: 155 us
  Pallas kernels  147 us (95%)
  local copies, waits for them, and re-layouts  3.87 us (2%)
  other arithmetic  3.43 us (2%)
    pallas_call x1, Pallas kernels, decode_step(): pl.pallas_call(functools.partial(step_kernel, levels, devices, frames, wi...  147 us
    unnamed x1, local copies, waits for them, and re-layouts  3.86 us

commit v1 on v0

v1 whole, which is shorter than its diff:
```python
import functools

import jax
import jax.numpy as jnp
from jax import lax
from jax.experimental import pallas as pl
from jax.experimental.pallas import tpu as pltpu
from jax.sharding import PartitionSpec as P

HEADS = 16
CORES = 2
LANES = 128
PAD = 16
MESH = pl.DeviceIdType.MESH


def layer_norm(values):
    centered = values - jnp.mean(values, axis=-1, keepdims=True)
    variance = jnp.mean(centered * centered, axis=-1, keepdims=True)
    return centered * lax.rsqrt(variance + 1e-05)


def dot_f32(left, right):
    return jnp.dot(left, right, preferred_element_type=jnp.float32)


def dot_nt(left, right):
    return lax.dot_general(left, right, (((1,), (1,)), ((), ())), preferred_element_type=jnp.float32)


def chip_at(position, chips):
    position = lax.rem(position + 2 * chips, chips)
    turned = position // (chips // 2)
    return (1 - turned) * 2 * position + turned * (2 * (chips - 1 - position) + 1)


def position_of(chip, chips):
    odd = lax.rem(chip, 2)
    return (1 - odd) * (chip // 2) + odd * (chips - 1 - chip // 2)


class Ring:
    def __init__(self, full, own, rows, chips, sems):
        self.full, self.own, self.rows, self.chips, self.half = full, own, rows, chips, chips // 2
        self.send, self.recv, self.sib_send, self.sib_recv = sems
        self.device = lax.axis_index("dp")
        self.core = lax.rem(self.device, CORES)
        self.position = position_of(self.device // CORES, chips)

    def block(self, position, core, part):
        row = (chip_at(position, self.chips) * CORES + core) * self.rows
        count = self.rows
        if part is not None:
            count = self.rows // 2
            row = row + part * count
        return self.full.at[pl.ds(pl.multiple_of(row, count), count), :]

    def own_block(self, part):
        if self.own is None:
            return self.block(self.position, self.core, part)
        if part is None:
            return self.own
        count = self.rows // 2
        return self.own.at[pl.ds(part * count, count), :]

    def part(self, way, step):
        return way if step == self.half - 1 else None

    def origin(self, way, step):
        return self.position - (1 + step) if way == 0 else self.position + (1 + step)

    def hop(self, way, step):
        towards = self.position + 1 if way == 0 else self.position - 1
        source = self.position - step if way == 0 else self.position + step
        part = self.part(way, step)
        place = self.block(source, self.core, part)
        target = chip_at(towards, self.chips) * CORES + self.core
        return pltpu.make_async_remote_copy(
            src_ref=self.own_block(part) if step == 0 else place,
            dst_ref=place,
            send_sem=self.send.at[way, step],
            recv_sem=self.recv.at[way, step],
            device_id={"dp": target},
            device_id_type=MESH,
        )

    def arrival(self, way, step):
        ref = self.block(self.origin(way, step), self.core, self.part(way, step))
        return pltpu.make_async_remote_copy(
            src_ref=ref,
            dst_ref=ref,
            send_sem=self.send.at[way, step],
            recv_sem=self.recv.at[way, step],
            device_id={"dp": self.device},
            device_id_type=MESH,
        )

    def share(self, way, step, core):
        position = self.position if step < 0 else self.origin(way, step)
        place = self.block(position, core, None if step < 0 else self.part(way, step))
        sibling = self.device + 1 - 2 * self.core
        return pltpu.make_async_remote_copy(
            src_ref=self.own_block(None) if step < 0 else place,
            dst_ref=place,
            send_sem=self.sib_send.at[way, step + 1],
            recv_sem=self.sib_recv.at[way, step + 1],
            device_id={"dp": sibling},
            device_id_type=MESH,
        )

    def start(self):
        for way in range(2):
            self.hop(way, 0).start()
        self.share(0, -1, self.core).start()

    def advance(self, step):
        for way in range(2):
            self.arrival(way, step).wait_recv()
            if step + 1 < self.half:
                self.hop(way, step + 1).start()
            self.share(way, step, self.core).start()

    def finish(self):
        for way in range(2):
            for step in range(self.half):
                self.hop(way, step).wait_send()
                self.share(way, step, self.core).wait_send()
                self.share(way, step, 1 - self.core).wait_recv()
        self.share(0, -1, self.core).wait_send()
        self.share(0, -1, 1 - self.core).wait_recv()


def step_kernel(
    levels, devices, frames, width,
    tok_ref, dec_ref, done_ref, fill_ref, table_ref, qkv_ref, out_ref, expand_ref, project_ref, depth_ref,
    final_ref,
    toks, decs, fills, ids, tables, proj, rest, embedded, keys, values_t, queries,
    attended, gated, final, scores_a, scores_b, peaks_a, peaks_b,
    local_sem, level_send, level_recv, table_send, table_recv, att_send, att_recv, final_sem,
    ring_a, ring_a_recv, sib_a, sib_a_recv, ring_b, ring_b_recv, sib_b, sib_b_recv,
):
    level = lax.axis_index("level")
    device = lax.axis_index("dp")
    core = lax.rem(device, CORES)
    sibling = device + 1 - 2 * core
    chips = devices // CORES
    rows = width // devices
    columns = width // levels
    codes = table_ref.shape[0]
    position = position_of(device // CORES, chips)
    bf16 = jnp.bfloat16

    barrier = pltpu.get_barrier_semaphore()
    for shift in range(1, levels):
        pl.semaphore_signal(barrier, inc=1, device_id={"level": lax.rem(level + shift, levels)}, device_id_type=MESH)
    for other in (
        sibling,
        chip_at(position + 1, chips) * CORES + core,
        chip_at(position - 1, chips) * CORES + core,
    ):
        pl.semaphore_signal(barrier, inc=1, device_id={"dp": other}, device_id_type=MESH)

    own_rows = pl.ds(pl.multiple_of(device * rows, rows), rows)
    own_columns = pl.ds(pl.multiple_of(level * columns, columns), columns)
    sources = (tok_ref, dec_ref, fill_ref, out_ref)

    def place_of(kind, owner):
        owner_columns = pl.ds(pl.multiple_of(owner * columns, columns), columns)
        return (toks.at[owner], decs.at[owner], fills.at[owner], rest.at[0, own_rows, owner_columns])[kind]

    def over_level(kind, shift):
        return pltpu.make_async_remote_copy(
            src_ref=sources[kind], dst_ref=place_of(kind, level),
            send_sem=level_send.at[kind, shift], recv_sem=level_recv.at[kind, shift],
            device_id={"level": lax.rem(level + shift, levels)}, device_id_type=MESH,
        )

    def from_level(kind, shift):
        sender = lax.rem(level + levels - shift, levels)
        return pltpu.make_async_remote_copy(
            src_ref=sources[kind], dst_ref=place_of(kind, sender),
            send_sem=level_send.at[kind, shift], recv_sem=level_recv.at[kind, shift],
            device_id={"level": sender}, device_id_type=MESH,
        )

    piece = LANES
    chunk = CORES * piece
    chunks = codes // chunk

    def chunk_rows(order, which):
        return pl.ds(pl.multiple_of((order * CORES + which) * piece, piece), piece)

    def table_out(order, shift):
        return pltpu.make_async_remote_copy(
            src_ref=table_ref.at[chunk_rows(order, core)], dst_ref=tables.at[level, chunk_rows(order, core)],
            send_sem=table_send.at[0, shift, order], recv_sem=table_recv.at[0, shift, order],
            device_id={"level": lax.rem(level + shift, levels)}, device_id_type=MESH,
        )

    def table_at(order, shift, which, kind):
        place = tables.at[lax.rem(level + levels - shift, levels), chunk_rows(order, which)]
        return pltpu.make_async_remote_copy(
            src_ref=place, dst_ref=place,
            send_sem=table_send.at[kind, shift, order], recv_sem=table_recv.at[kind, shift, order],
            device_id={"dp": sibling}, device_id_type=MESH,
        )

    early = [
        pltpu.make_async_copy(sources[kind], place_of(kind, level), local_sem.at[kind]) for kind in range(3)
    ] + [pltpu.make_async_copy(table_ref, tables.at[level], local_sem.at[3])]
    late = [
        pltpu.make_async_copy(qkv_ref.at[part], proj.at[part, own_rows, :], local_sem.at[4 + part]) for part in range(3)
    ] + [
        pltpu.make_async_copy(out_ref, place_of(3, level), local_sem.at[7]),
        pltpu.make_async_copy(expand_ref.at[:, pl.ds(0, width)], rest.at[1, own_rows, :], local_sem.at[8]),
        pltpu.make_async_copy(expand_ref.at[:, pl.ds(width, width)], rest.at[2, own_rows, :], local_sem.at[9]),
        pltpu.make_async_copy(project_ref, rest.at[3, own_rows, :], local_sem.at[10]),
    ]
    for copy in early + late:
        copy.start()

    def rings(full, own, count, sems):
        return [
            Ring(full.at[part], own(part), rows, chips, tuple(sem.at[part] for sem in sems))
            for part in range(count)
        ]

    first = rings(proj, lambda part: qkv_ref.at[part], 3, (ring_a, ring_a_recv, sib_a, sib_a_recv))
    second = rings(rest, lambda part: None, 4, (ring_b, ring_b_recv, sib_b, sib_b_recv))
    hops = chips // 2

    pl.semaphore_wait(barrier, levels + 2)
    for kind in range(3):
        for shift in range(1, levels):
            over_level(kind, shift).start()
    for ring in first:
        ring.start()
    for order in range(chunks):
        for shift in range(1, levels):
            table_out(order, shift).start()
        if order == 0:
            for shift in range(1, levels):
                over_level(3, shift).start()

    for pair in range(values_t.shape[0]):
        values_t[pair, LANES:, :] = jnp.ones((values_t.shape[1] - LANES, frames), bf16)
    for place in (pl.ds(0, PAD), pl.ds(PAD + frames, PAD)):
        gated[place, :] = jnp.zeros((PAD, width), bf16)

    for copy in early:
        copy.wait()
    for kind in range(3):
        for shift in range(1, levels):
            from_level(kind, shift).wait_recv()

    done = done_ref[0]
    for row in range(levels):
        use = (row < done) | ((row == done) & (decs[row] == 1))
        code = jnp.where(use, toks[row], -1).astype(jnp.float32)
        for base in range(0, frames, LANES):
            ids[row, base : base + LANES, :] = jnp.broadcast_to(code[:, base : base + LANES], (LANES, LANES)).T

    tile = 2 * LANES
    tiles = frames // tile
    lane = lax.broadcasted_iota(jnp.int32, (tile, LANES), 1).astype(jnp.float32)

    def span_of(step):
        return pl.ds(pl.multiple_of(step * tile, tile), tile)

    def onehot(found, start, count):
        return jnp.concatenate(
            [jnp.where(found - start == lane + float(base), 1.0, 0.0).astype(bf16) for base in range(0, count, LANES)],
            axis=1,
        )

    @pl.loop(0, tiles)
    def _(step):
        @pl.when(step == tiles // 2)
        def _():
            for ring in first:
                ring.advance(0)

        span = span_of(step)
        total = dot_f32(onehot(ids[level, span, :], 0.0, codes), tables[level])
        for row in range(levels):
            total = total + jnp.where(ids[row, span, 0:1] < 0.0, fills[row].astype(jnp.float32), 0.0)
        embedded[span, :] = total

    @pl.loop(0, chunks)
    def _(order):
        begin = (order * chunk).astype(jnp.float32)
        codes_at = pl.ds(pl.multiple_of(order * chunk, chunk), chunk)
        for shift in range(1, levels):
            sender = lax.rem(level + levels - shift, levels)
            table_at(order, shift, core, 0).wait_recv()
            table_at(order, shift, core, 1).start()
            table_at(order, shift, 1 - core, 1).wait_recv()

            @pl.loop(0, tiles)
            def _(step):
                span = span_of(step)
                found = onehot(ids[sender, span, :], begin, chunk)
                embedded[span, :] = embedded[span, :] + dot_f32(found, tables[sender, codes_at, :])

        for step in range(1, hops):
            @pl.when(order == (step - 1) * chunks // (hops - 1))
            def _():
                for ring in first:
                    ring.advance(step)
                if step == max(hops - 2, 1):
                    for copy in late:
                        copy.wait()
                    for shift in range(1, levels):
                        from_level(3, shift).wait_recv()
                    for ring in second:
                        ring.start()

    for ring in first:
        ring.finish()

    head_dim = width // HEADS
    scale = head_dim ** (-0.5)
    pairs = columns // LANES

    @pl.loop(0, tiles)
    def _(step):
        for part, ring in enumerate(second):
            @pl.when(step == min(max(2 * part - 2, 0), tiles - 1))
            def _():
                ring.advance(0)

        span = span_of(step)
        normed = layer_norm(embedded[span, :]).astype(bf16)
        queries[span, :] = dot_f32(normed, proj[0]).astype(bf16) * jnp.asarray(scale, bf16)
        keys[span, :] = dot_f32(normed, proj[1]).astype(bf16)
        found = dot_f32(normed, proj[2])
        for pair in range(pairs):
            values_t[pair, 0:LANES, span] = found[:, pair * LANES : (pair + 1) * LANES].T.astype(bf16)

    block = LANES
    stages = frames // block

    def rows_of(stage):
        return pl.ds(pl.multiple_of(stage * block, block), block)

    def attended_copy(stage, shift, owner, target):
        owner_columns = pl.ds(pl.multiple_of(owner * columns, columns), columns)
        place = attended.at[rows_of(stage), owner_columns]
        return pltpu.make_async_remote_copy(
            src_ref=place, dst_ref=place,
            send_sem=att_send.at[stage, shift], recv_sem=att_recv.at[stage, shift],
            device_id={"level": target}, device_id_type=MESH,
        )

    def attended_out(stage, shift):
        return attended_copy(stage, shift, level, lax.rem(level + shift, levels))

    def attended_in(stage, shift):
        sender = lax.rem(level + levels - shift, levels)
        return attended_copy(stage, shift, sender, sender)

    lower = lax.broadcasted_iota(jnp.int32, (block, LANES), 1) < head_dim
    buffers = ((scores_a, peaks_a), (scores_b, peaks_b))

    def score_pair(stage, pair, buffer):
        store, peaks = buffer
        across = pl.ds(pair * LANES, LANES)
        query = queries[rows_of(stage), across]
        zero = jnp.zeros_like(query)
        both = jnp.concatenate([jnp.where(lower, query, zero), jnp.where(lower, zero, query)], axis=0)
        found = dot_nt(keys[:, across], both)
        store[...] = found
        peaks[...] = jnp.max(found.reshape(frames // 8, 8, CORES * block), axis=0)

    def mix_pair(stage, pair, buffer):
        store, peaks = buffer
        peak = jnp.max(peaks[...], axis=0, keepdims=True)
        weights = jnp.exp(store[...] - peak).astype(bf16)
        mixed = dot_f32(values_t[pair], weights)
        inverse = 1.0 / mixed[LANES : LANES + 1, :]
        low = mixed[0:head_dim, 0:block] * inverse[:, 0:block]
        high = mixed[head_dim : 2 * head_dim, block:] * inverse[:, block:]
        across = pl.ds(pl.multiple_of(level * columns + pair * LANES, LANES), LANES)
        attended[rows_of(stage), across] = jnp.concatenate([low, high], axis=0).T.astype(bf16)

    per_turn = 1 if pairs % 2 == 0 else 2
    units = [(ahead, pair) for ahead in range(per_turn) for pair in range(pairs)]
    events = [(step, ring) for step in range(1, hops) for ring in second]
    turns = stages // per_turn

    score_pair(0, 0, buffers[0])

    @pl.loop(0, turns)
    def _(turn):
        for event, (step, ring) in enumerate(events):
            @pl.when(turn == event * turns // len(events))
            def _():
                ring.advance(step)

        @pl.when(turn > 0)
        def _():
            for ahead in range(per_turn):
                for shift in range(1, levels):
                    attended_out((turn - 1) * per_turn + ahead, shift).start()

        for index, (ahead, pair) in enumerate(units):
            if index + 1 < len(units):
                next_ahead, next_pair = units[index + 1]
                next_stage = turn * per_turn + next_ahead
            else:
                next_pair = 0
                next_stage = lax.min((turn + 1) * per_turn, stages - 1)
            score_pair(next_stage, next_pair, buffers[(index + 1) % 2])
            mix_pair(turn * per_turn + ahead, pair, buffers[index % 2])

    for ahead in range(per_turn):
        for shift in range(1, levels):
            attended_out((turns - 1) * per_turn + ahead, shift).start()
    for ring in second:
        ring.finish()

    taps = depth_ref.shape[0]
    depth = depth_ref[...].astype(jnp.float32)

    def gate(step):
        for ahead in range(tile // block):
            for shift in range(1, levels):
                attended_in(step * (tile // block) + ahead, shift).wait_recv()
        span = span_of(step)
        after_attn = embedded[span, :] + dot_nt(attended[span, :], rest[0])
        embedded[span, :] = after_attn
        normed = layer_norm(after_attn).astype(bf16)
        mixed = dot_f32(normed, rest[1]) * jax.nn.sigmoid(dot_f32(normed, rest[2]))
        gated[pl.ds(pl.multiple_of(PAD + step * tile, PAD), tile), :] = mixed.astype(bf16)

    def final_copy(step):
        span = span_of(step)
        return pltpu.make_async_copy(final.at[span], final_ref.at[span], final_sem.at[step])

    def convolve(step):
        span = span_of(step)
        start = pl.multiple_of(step * tile, tile)
        window = gated[pl.ds(start, tile + 2 * PAD), :].astype(jnp.float32)
        conv = jnp.zeros((tile, width), jnp.float32)
        for tap in range(taps):
            first_row = PAD - taps // 2 + tap
            conv = conv + window[first_row : first_row + tile] * depth[tap : tap + 1, :]
        activated = (conv * jax.nn.sigmoid(conv)).astype(bf16)
        after_conv = embedded[span, :] + dot_f32(activated, rest[3])
        final[span, :] = layer_norm(after_conv).astype(bf16)
        final_copy(step).start()

    gate(0)

    @pl.loop(0, tiles - 1)
    def _(step):
        gate(step + 1)
        convolve(step)

    convolve(tiles - 1)

    for shift in range(1, levels):
        for kind in range(4):
            over_level(kind, shift).wait_send()

        @pl.loop(0, chunks)
        def _(order):
            table_out(order, shift).wait_send()
            table_at(order, shift, core, 1).wait_send()

        @pl.loop(0, stages)
        def _(stage):
            attended_out(stage, shift).wait_send()

    @pl.loop(0, tiles)
    def _(step):
        final_copy(step).wait()


def decode_step(levels, devices, tokens, decoded, done, fill, table, w_qkv, w_out_t, w_expand, w_project, taps):
    frames, width = tokens.shape[1], table.shape[1]
    chips = devices // CORES
    columns = width // levels
    chunks = table.shape[0] // (CORES * LANES)
    stages = frames // LANES
    tiles = frames // (2 * LANES)
    vmem = pl.BlockSpec(memory_space=pltpu.VMEM)
    anywhere = pl.BlockSpec(memory_space=pl.ANY)
    dma = pltpu.SemaphoreType.DMA
    half = chips // 2
    bf16, f32 = jnp.bfloat16, jnp.float32
    return pl.pallas_call(
        functools.partial(step_kernel, levels, devices, frames, width),
        out_shape=jax.ShapeDtypeStruct((frames, width), bf16),
        in_specs=[anywhere] * 2 + [pl.BlockSpec(memory_space=pltpu.SMEM)] + [anywhere] * 6 + [vmem],
        out_specs=anywhere,
        scratch_shapes=[
            pltpu.VMEM((levels,) + tokens.shape, jnp.int32),
            pltpu.VMEM((levels,) + decoded.shape, jnp.int32),
            pltpu.VMEM((levels,) + fill.shape, bf16),
            pltpu.VMEM((levels, frames, LANES), f32),
            pltpu.VMEM((levels,) + table.shape, bf16),
            pltpu.VMEM((3, width, columns), bf16),
            pltpu.VMEM((4, width, width), bf16),
            pltpu.VMEM((frames, width), f32),
            pltpu.VMEM((frames, columns), bf16),
            pltpu.VMEM((columns // LANES, LANES + 16, frames), bf16),
            pltpu.VMEM((frames, columns), bf16),
            pltpu.VMEM((frames, width), bf16),
            pltpu.VMEM((frames + 2 * PAD, width), bf16),
            pltpu.VMEM((frames, width), bf16),
            pltpu.VMEM((frames, 2 * LANES), f32),
            pltpu.VMEM((frames, 2 * LANES), f32),
            pltpu.VMEM((8, 2 * LANES), f32),
            pltpu.VMEM((8, 2 * LANES), f32),
            dma((11,)),
            dma((4, levels)), dma((4, levels)), dma((2, levels, chunks)), dma((2, levels, chunks)),
            dma((stages, levels)), dma((stages, levels)), dma((tiles,)),
        ]
        + [
            dma((count, 2, half + extra)) for count in (3, 4) for extra in (0, 0, 1, 1)
        ],
        compiler_params=pltpu.CompilerParams(
            collective_id=0, has_side_effects=True, vmem_limit_bytes=64000 * 1024
        ),
    )(tokens, decoded, done, fill, table, w_qkv, w_out_t, w_expand, w_project, taps)


def body(
    token_ids,
    decoded_mask,
    levels_done,
    code_tables,
    mask_vectors,
    w_qkv,
    w_out,
    w_expand,
    w_depth,
    w_project,
    level_heads,
):
    final = decode_step(
        lax.axis_size("level"), lax.axis_size("dp"), token_ids[0], decoded_mask[0], levels_done, mask_vectors,
        code_tables[0], w_qkv, w_out.T, w_expand, w_project, w_depth,
    )
    return dot_f32(final, level_heads[0]).astype(jnp.bfloat16)[None, None]


def solution(mesh):
    return jax.shard_map(
        body,
        mesh=mesh,
        in_specs=(
            P("dp", "level", None),
            P("dp", "level", None),
            P("dp"),
            P("level", None, None),
            P("level", None),
            P(None, "dp", "level"),
            P("level", "dp"),
            P("dp", None),
            P(),
            P("dp", None),
            P("level", None, None),
        ),
        out_specs=P("dp", "level", None, None),
        check_vma=False,
    )
```

time: 155 us -> 109 us (0.70)
  Pallas kernels: 147 us -> 99.1 us
  matrix products: 0 us -> 7.65 us
  local copies, waits for them, and re-layouts: 3.87 us -> 0 us
  other arithmetic: 3.43 us -> 0 us
    pallas_call x1, Pallas kernels: 147 us -> 99.1 us  [decode_step(): pl.pallas_call(functools.partial(step_kernel, levels, devices, frames, wi...]
    dot_general x0 -> x1, matrix products: none -> 7.65 us  [dot_f32(): return jnp.dot(left, right, preferred_element_type=jnp.float32)]
    unnamed x1 -> x0, local copies, waits for them, and re-layouts: 3.86 us -> none
    convert_element_type x2 -> x0, other arithmetic: 2.06 us -> none  [the longest x1 1.32 us: body(): w_depth.astype(jnp.float32)]
where the time goes in v1:
time: 109 us; the launch traced here: 107 us
  Pallas kernels  99.1 us (91%)
  matrix products  7.65 us (7%)
    pallas_call x1, Pallas kernels, decode_step(): pl.pallas_call(functools.partial(step_kernel, levels, devices, frames, wi...  99.1 us
    dot_general x1, matrix products, dot_f32(): return jnp.dot(left, right, preferred_element_type=jnp.float32)  7.65 us

profile of v1, /device:TPU:0, one launch (start us, length us, event | category | flops | bytes accessed | tf_op | source)
XLA Modules:
  0.0 107.4 jit_solution(15980551953219413346)
XLA Ops:
  0.7 99.1 %shard_map.109 = bf16[1536,1024]{1,0:T(8,128)(2,1)} custom-call(s32[1,1536]{1,0:T(1,128)} %bitcast.12, s32[1,1536]{1,0:T(1,128)} %bitcast.13, s32[1]{0:T(128)S(6)} %copy.12.done_ref, bf16[1,1024]{1,0:T(2,128)(2,1)} %fill_ref.1, bf16[1024,1024]{1,0:T(8,128)(2,1)} %bitcast.10, bf16[3,64,512]{2,1,0:T(8,128)(2,1)} %qkv_ref.1, bf16[64,512]{1,0:T(8,128)(2,1)} %bitcast.11, ...), custom_call_target="tpu_custom_call" | custom-call | tf_op jit(solution)/shard_map/pallas_call | solution.py:492
  99.8 7.6 %fusion = bf16[1,1,1536,1024]{3,2,1,0:T(8,128)(2,1)} fusion(bf16[1536,1024]{1,0:T(8,128)(2,1)} %shard_map.109, bf16[1,1024,1024]{2,1,0:T(8,128)(2,1)} %param.21), kind=kOutput, calls=%fused_computation.1 | convolution fusion | flops 3222798336 | bytes 8388608 | tf_op jit(solution)/shard_map/dot_general | solution.py:24

commit v2 on v1

--- a/solution.py
+++ b/solution.py
@@ -78,7 +78,7 @@
         return pltpu.make_async_remote_copy(
             src_ref=self.own_block(part) if step == 0 else place,
             dst_ref=place,
-            send_sem=self.send.at[way, step],
+            send_sem=self.send,
             recv_sem=self.recv.at[way, step],
             device_id={"dp": target},
             device_id_type=MESH,
@@ -89,7 +89,7 @@
         return pltpu.make_async_remote_copy(
             src_ref=ref,
             dst_ref=ref,
-            send_sem=self.send.at[way, step],
+            send_sem=self.send,
             recv_sem=self.recv.at[way, step],
             device_id={"dp": self.device},
             device_id_type=MESH,
@@ -102,8 +102,8 @@
         return pltpu.make_async_remote_copy(
             src_ref=self.own_block(None) if step < 0 else place,
             dst_ref=place,
-            send_sem=self.sib_send.at[way, step + 1],
-            recv_sem=self.sib_recv.at[way, step + 1],
+            send_sem=self.sib_send,
+            recv_sem=self.sib_recv,
             device_id={"dp": sibling},
             device_id_type=MESH,
         )
@@ -120,14 +120,22 @@
                 self.hop(way, step + 1).start()
             self.share(way, step, self.core).start()
 
+    def all_of(self, blocks, send, recv):
+        ref = self.full.at[pl.ds(0, blocks * self.rows), :]
+        return pltpu.make_async_remote_copy(
+            src_ref=ref,
+            dst_ref=ref,
+            send_sem=send,
+            recv_sem=recv,
+            device_id={"dp": self.device},
+            device_id_type=MESH,
+        )
+
     def finish(self):
-        for way in range(2):
-            for step in range(self.half):
-                self.hop(way, step).wait_send()
-                self.share(way, step, self.core).wait_send()
-                self.share(way, step, 1 - self.core).wait_recv()
-        self.share(0, -1, self.core).wait_send()
-        self.share(0, -1, 1 - self.core).wait_recv()
+        self.all_of(self.chips - 1, self.send, self.sib_recv).wait_send()
+        shared = self.all_of(self.chips, self.sib_send, self.sib_recv)
+        shared.wait_send()
+        shared.wait_recv()
 
 
 def step_kernel(
@@ -135,7 +143,7 @@
     tok_ref, dec_ref, done_ref, fill_ref, table_ref, qkv_ref, out_ref, expand_ref, project_ref, depth_ref,
     final_ref,
     toks, decs, fills, ids, tables, proj, rest, embedded, keys, values_t, queries,
-    attended, gated, final, scores_a, scores_b, peaks_a, peaks_b,
+    normed_a, normed_b, attended, gated, final, scores_a, scores_b, peaks_a, peaks_b,
     local_sem, level_send, level_recv, table_send, table_recv, att_send, att_recv, final_sem,
     ring_a, ring_a_recv, sib_a, sib_a_recv, ring_b, ring_b_recv, sib_b, sib_b_recv,
 ):
@@ -193,7 +201,7 @@
     def table_out(order, shift):
         return pltpu.make_async_remote_copy(
             src_ref=table_ref.at[chunk_rows(order, core)], dst_ref=tables.at[level, chunk_rows(order, core)],
-            send_sem=table_send.at[0, shift, order], recv_sem=table_recv.at[0, shift, order],
+            send_sem=table_send.at[0, shift], recv_sem=table_recv.at[0, shift, order],
             device_id={"level": lax.rem(level + shift, levels)}, device_id_type=MESH,
         )
 
@@ -201,7 +209,7 @@
         place = tables.at[lax.rem(level + levels - shift, levels), chunk_rows(order, which)]
         return pltpu.make_async_remote_copy(
             src_ref=place, dst_ref=place,
-            send_sem=table_send.at[kind, shift, order], recv_sem=table_recv.at[kind, shift, order],
+            send_sem=table_send.at[kind, shift], recv_sem=table_recv.at[kind, shift, order],
             device_id={"dp": sibling}, device_id_type=MESH,
         )
 
@@ -226,8 +234,39 @@
         ]
 
     first = rings(proj, lambda part: qkv_ref.at[part], 3, (ring_a, ring_a_recv, sib_a, sib_a_recv))
-    second = rings(rest, lambda part: None, 4, (ring_b, ring_b_recv, sib_b, sib_b_recv))
+    rest_sources = (
+        None, expand_ref.at[:, pl.ds(0, width)], expand_ref.at[:, pl.ds(width, width)], project_ref,
+    )
+    second = rings(rest, lambda part: rest_sources[part], 4, (ring_b, ring_b_recv, sib_b, sib_b_recv))
     hops = chips // 2
+    turn = (1, 2, 0, 3)
+    slots = ("c1", "c2", "c3", "c3", "q0", "q1", "s0", "s1", "s2", "s2", "s3", "s4", "s4", "s5", "s5", "end")
+    plan = {}
+
+    def at_slot(slot, act):
+        plan.setdefault(slot, []).append(act)
+
+    def run(slot):
+        for act in plan.get(slot, ()):
+            act()
+
+    def start_second(part):
+        if part == 0:
+            for copy in late:
+                copy.wait()
+            for shift in range(1, levels):
+                from_level(3, shift).wait_recv()
+        second[part].start()
+
+    for step in range(hops):
+        slot = ("e", "c0", "c1", "c2")[step * 4 // hops]
+        for ring in first:
+            at_slot(slot, functools.partial(ring.advance, step))
+    for slot, part in zip(("start", "e", "c0", "c1"), turn):
+        at_slot(slot, functools.partial(start_second, part))
+    order_of = [(step, part) for step in range(hops) for part in turn]
+    for index, (step, part) in enumerate(order_of):
+        at_slot(slots[index * len(slots) // len(order_of)], functools.partial(second[part].advance, step))
 
     pl.semaphore_wait(barrier, levels + 2)
     for kind in range(3):
@@ -235,15 +274,17 @@
             over_level(kind, shift).start()
     for ring in first:
         ring.start()
+    run("start")
+    for shift in range(1, levels):
+        over_level(3, shift).start()
     for order in range(chunks):
         for shift in range(1, levels):
             table_out(order, shift).start()
-        if order == 0:
-            for shift in range(1, levels):
-                over_level(3, shift).start()
-
-    for pair in range(values_t.shape[0]):
-        values_t[pair, LANES:, :] = jnp.ones((values_t.shape[1] - LANES, frames), bf16)
+
+    head_dim = width // HEADS
+    heads = columns // head_dim
+    for head in range(heads):
+        values_t[head, head_dim:, :] = jnp.ones((values_t.shape[1] - head_dim, frames), bf16)
     for place in (pl.ds(0, PAD), pl.ds(PAD + frames, PAD)):
         gated[place, :] = jnp.zeros((PAD, width), bf16)
 
@@ -277,8 +318,7 @@
     def _(step):
         @pl.when(step == tiles // 2)
         def _():
-            for ring in first:
-                ring.advance(0)
+            run("e")
 
         span = span_of(step)
         total = dot_f32(onehot(ids[level, span, :], 0.0, codes), tables[level])
@@ -286,69 +326,84 @@
             total = total + jnp.where(ids[row, span, 0:1] < 0.0, fills[row].astype(jnp.float32), 0.0)
         embedded[span, :] = total
 
-    @pl.loop(0, chunks)
+    def receive(order, shift):
+        table_at(order, shift, core, 0).wait_recv()
+        table_at(order, shift, core, 1).start()
+        table_at(order, shift, 1 - core, 1).wait_recv()
+
+    def picked(order, shift, span):
+        sender = lax.rem(level + levels - shift, levels)
+        found = onehot(ids[sender, span, :], lax.convert_element_type(order * chunk, jnp.float32), chunk)
+        return dot_f32(found, tables[sender, pl.ds(pl.multiple_of(order * chunk, chunk), chunk), :])
+
+    def add_chunk(order, shift):
+        receive(order, shift)
+
+        @pl.loop(0, tiles)
+        def _(step):
+            span = span_of(step)
+            embedded[span, :] = embedded[span, :] + picked(order, shift, span)
+
+    @pl.loop(0, chunks - 1)
     def _(order):
-        begin = (order * chunk).astype(jnp.float32)
-        codes_at = pl.ds(pl.multiple_of(order * chunk, chunk), chunk)
         for shift in range(1, levels):
-            sender = lax.rem(level + levels - shift, levels)
-            table_at(order, shift, core, 0).wait_recv()
-            table_at(order, shift, core, 1).start()
-            table_at(order, shift, 1 - core, 1).wait_recv()
-
-            @pl.loop(0, tiles)
-            def _(step):
-                span = span_of(step)
-                found = onehot(ids[sender, span, :], begin, chunk)
-                embedded[span, :] = embedded[span, :] + dot_f32(found, tables[sender, codes_at, :])
-
-        for step in range(1, hops):
-            @pl.when(order == (step - 1) * chunks // (hops - 1))
+            add_chunk(order, shift)
+        for quarter in range(3):
+            @pl.when(order == quarter * (chunks - 1) // 3)
             def _():
-                for ring in first:
-                    ring.advance(step)
-                if step == max(hops - 2, 1):
-                    for copy in late:
-                        copy.wait()
-                    for shift in range(1, levels):
-                        from_level(3, shift).wait_recv()
-                    for ring in second:
-                        ring.start()
-
+                run(f"c{quarter}")
+
+    last = jnp.int32(chunks - 1)
+    for shift in range(1, levels - 1):
+        add_chunk(last, shift)
+    receive(last, levels - 1)
     for ring in first:
         ring.finish()
-
-    head_dim = width // HEADS
+    run("c3")
+
     scale = head_dim ** (-0.5)
-    pairs = columns // LANES
-
-    @pl.loop(0, tiles)
-    def _(step):
-        for part, ring in enumerate(second):
-            @pl.when(step == min(max(2 * part - 2, 0), tiles - 1))
+
+    def prepare(step, normed):
+        span = span_of(step)
+        total = embedded[span, :] + picked(last, levels - 1, span)
+        embedded[span, :] = total
+        normed[...] = layer_norm(total).astype(bf16)
+
+    def project(step, normed):
+        span = span_of(step)
+        queries[span, :] = dot_f32(normed[...], proj[0]).astype(bf16) * jnp.asarray(scale, bf16)
+        keys[span, :] = dot_f32(normed[...], proj[1]).astype(bf16)
+        found = dot_f32(normed[...], proj[2])
+        for pair in range(heads // 2):
+            turned = found[:, pair * LANES : (pair + 1) * LANES].T.astype(bf16)
+            values_t[2 * pair, 0:head_dim, span] = turned[0:head_dim]
+            values_t[2 * pair + 1, 0:head_dim, span] = turned[head_dim:]
+
+    prepare(0, normed_a)
+
+    @pl.loop(0, tiles // 2)
+    def _(half):
+        for quarter in range(2):
+            @pl.when(half == min(1 + quarter, tiles // 2 - 1))
             def _():
-                ring.advance(0)
-
-        span = span_of(step)
-        normed = layer_norm(embedded[span, :]).astype(bf16)
-        queries[span, :] = dot_f32(normed, proj[0]).astype(bf16) * jnp.asarray(scale, bf16)
-        keys[span, :] = dot_f32(normed, proj[1]).astype(bf16)
-        found = dot_f32(normed, proj[2])
-        for pair in range(pairs):
-            values_t[pair, 0:LANES, span] = found[:, pair * LANES : (pair + 1) * LANES].T.astype(bf16)
-
-    block = LANES
-    stages = frames // block
-
-    def rows_of(stage):
-        return pl.ds(pl.multiple_of(stage * block, block), block)
+                run(f"q{quarter}")
+
+        step = 2 * half
+        project(step, normed_a)
+        prepare(step + 1, normed_b)
+
+        project(step + 1, normed_b)
+
+        @pl.when(half < tiles // 2 - 1)
+        def _():
+            prepare(step + 2, normed_a)
 
     def attended_copy(stage, shift, owner, target):
         owner_columns = pl.ds(pl.multiple_of(owner * columns, columns), columns)
-        place = attended.at[rows_of(stage), owner_columns]
+        place = attended.at[span_of(stage), owner_columns]
         return pltpu.make_async_remote_copy(
             src_ref=place, dst_ref=place,
-            send_sem=att_send.at[stage, shift], recv_sem=att_recv.at[stage, shift],
+            send_sem=att_send.at[shift], recv_sem=att_recv.at[stage, shift],
             device_id={"level": target}, device_id_type=MESH,
         )
 
@@ -359,63 +414,62 @@
         sender = lax.rem(level + levels - shift, levels)
         return attended_copy(stage, shift, sender, sender)
 
-    lower = lax.broadcasted_iota(jnp.int32, (block, LANES), 1) < head_dim
+    lower = lax.broadcasted_iota(jnp.int32, (tile, LANES), 1) < head_dim
+    part = frames // 2
     buffers = ((scores_a, peaks_a), (scores_b, peaks_b))
 
-    def score_pair(stage, pair, buffer):
-        store, peaks = buffer
-        across = pl.ds(pair * LANES, LANES)
-        query = queries[rows_of(stage), across]
+    def masked_query(stage, head):
+        query = queries[span_of(stage), pl.ds(head // 2 * LANES, LANES)]
         zero = jnp.zeros_like(query)
-        both = jnp.concatenate([jnp.where(lower, query, zero), jnp.where(lower, zero, query)], axis=0)
-        found = dot_nt(keys[:, across], both)
-        store[...] = found
-        peaks[...] = jnp.max(found.reshape(frames // 8, 8, CORES * block), axis=0)
-
-    def mix_pair(stage, pair, buffer):
-        store, peaks = buffer
-        peak = jnp.max(peaks[...], axis=0, keepdims=True)
-        weights = jnp.exp(store[...] - peak).astype(bf16)
-        mixed = dot_f32(values_t[pair], weights)
-        inverse = 1.0 / mixed[LANES : LANES + 1, :]
-        low = mixed[0:head_dim, 0:block] * inverse[:, 0:block]
-        high = mixed[head_dim : 2 * head_dim, block:] * inverse[:, block:]
-        across = pl.ds(pl.multiple_of(level * columns + pair * LANES, LANES), LANES)
-        attended[rows_of(stage), across] = jnp.concatenate([low, high], axis=0).T.astype(bf16)
-
-    per_turn = 1 if pairs % 2 == 0 else 2
-    units = [(ahead, pair) for ahead in range(per_turn) for pair in range(pairs)]
-    events = [(step, ring) for step in range(1, hops) for ring in second]
-    turns = stages // per_turn
-
-    score_pair(0, 0, buffers[0])
-
-    @pl.loop(0, turns)
-    def _(turn):
-        for event, (step, ring) in enumerate(events):
-            @pl.when(turn == event * turns // len(events))
+        return jnp.where(lower, query, zero) if head % 2 == 0 else jnp.where(lower, zero, query)
+
+    def score_part(query, head, buffer, begin, count):
+        found = dot_nt(keys[begin : begin + count, head // 2 * LANES : (head // 2 + 1) * LANES], query)
+        buffer[0][begin : begin + count, :] = found
+        return jnp.max(found.reshape(count // 8, 8, tile), axis=0)
+
+    def mix_part(head, buffer, peak, begin, count):
+        weights = jnp.exp(buffer[0][begin : begin + count, :] - peak).astype(bf16)
+        return dot_f32(values_t[head, :, begin : begin + count], weights)
+
+    def attend(stage, head, buffer, next_stage, next_head, next_buffer):
+        query = masked_query(next_stage, next_head)
+        peak = jnp.max(buffer[1][...], axis=0, keepdims=True)
+        top, mixed = [], []
+        for begin in range(0, frames, part):
+            top.append(score_part(query, next_head, next_buffer, begin, part))
+            mixed.append(mix_part(head, buffer, peak, begin, part))
+        next_buffer[1][...] = jnp.maximum(top[0], top[1])
+        total = mixed[0] + mixed[1]
+        return total[0:head_dim] * (1.0 / total[head_dim : head_dim + 1])
+
+    peaks_a[...] = score_part(masked_query(0, 0), 0, buffers[0], 0, frames)
+
+    @pl.loop(0, tiles)
+    def _(stage):
+        for sixth in range(6):
+            @pl.when(stage == sixth * tiles // 6)
             def _():
-                ring.advance(step)
-
-        @pl.when(turn > 0)
+                run(f"s{sixth}")
+
+        @pl.when(stage > 0)
         def _():
-            for ahead in range(per_turn):
-                for shift in range(1, levels):
-                    attended_out((turn - 1) * per_turn + ahead, shift).start()
-
-        for index, (ahead, pair) in enumerate(units):
-            if index + 1 < len(units):
-                next_ahead, next_pair = units[index + 1]
-                next_stage = turn * per_turn + next_ahead
+            for shift in range(1, levels):
+                attended_out(stage - 1, shift).start()
+
+        low = None
+        for head in range(heads):
+            ahead = (stage, head + 1) if head + 1 < heads else (lax.min(stage + 1, tiles - 1), 0)
+            found = attend(stage, head, buffers[head % 2], *ahead, buffers[(head + 1) % 2])
+            if head % 2 == 0:
+                low = found
             else:
-                next_pair = 0
-                next_stage = lax.min((turn + 1) * per_turn, stages - 1)
-            score_pair(next_stage, next_pair, buffers[(index + 1) % 2])
-            mix_pair(turn * per_turn + ahead, pair, buffers[index % 2])
-
-    for ahead in range(per_turn):
-        for shift in range(1, levels):
-            attended_out((turns - 1) * per_turn + ahead, shift).start()
+                across = pl.ds(pl.multiple_of(level * columns + head // 2 * LANES, LANES), LANES)
+                attended[span_of(stage), across] = jnp.concatenate([low, found], axis=0).T.astype(bf16)
+
+    for shift in range(1, levels):
+        attended_out(tiles - 1, shift).start()
+    run("end")
     for ring in second:
         ring.finish()
 
@@ -423,9 +477,8 @@
     depth = depth_ref[...].astype(jnp.float32)
 
     def gate(step):
-        for ahead in range(tile // block):
-            for shift in range(1, levels):
-                attended_in(step * (tile // block) + ahead, shift).wait_recv()
+        for shift in range(1, levels):
+            attended_in(step, shift).wait_recv()
         span = span_of(step)
         after_attn = embedded[span, :] + dot_nt(attended[span, :], rest[0])
         embedded[span, :] = after_attn
@@ -435,7 +488,7 @@
 
     def final_copy(step):
         span = span_of(step)
-        return pltpu.make_async_copy(final.at[span], final_ref.at[span], final_sem.at[step])
+        return pltpu.make_async_copy(final.at[span], final_ref.at[span], final_sem.at[0])
 
     def convolve(step):
         span = span_of(step)
@@ -451,30 +504,35 @@
         final_copy(step).start()
 
     gate(0)
-
-    @pl.loop(0, tiles - 1)
+    gate(1)
+
+    @pl.loop(0, tiles - 2)
     def _(step):
-        gate(step + 1)
         convolve(step)
-
+        gate(step + 2)
+
+    convolve(tiles - 2)
     convolve(tiles - 1)
 
     for shift in range(1, levels):
         for kind in range(4):
             over_level(kind, shift).wait_send()
 
-        @pl.loop(0, chunks)
-        def _(order):
-            table_out(order, shift).wait_send()
-            table_at(order, shift, core, 1).wait_send()
-
-        @pl.loop(0, stages)
-        def _(stage):
-            attended_out(stage, shift).wait_send()
-
-    @pl.loop(0, tiles)
-    def _(step):
-        final_copy(step).wait()
+        sent = tables.at[level, pl.ds(0, codes // CORES)]
+        for kind in range(2):
+            pltpu.make_async_remote_copy(
+                src_ref=sent, dst_ref=sent,
+                send_sem=table_send.at[kind, shift], recv_sem=table_recv.at[kind, shift, 0],
+                device_id={"level": level}, device_id_type=MESH,
+            ).wait_send()
+        sent = attended.at[:, own_columns]
+        pltpu.make_async_remote_copy(
+            src_ref=sent, dst_ref=sent,
+            send_sem=att_send.at[shift], recv_sem=att_recv.at[0, shift],
+            device_id={"level": level}, device_id_type=MESH,
+        ).wait_send()
+
+    pltpu.make_async_copy(final, final_ref, final_sem.at[0]).wait()
 
 
 def decode_step(levels, devices, tokens, decoded, done, fill, table, w_qkv, w_out_t, w_expand, w_project, taps):
@@ -482,7 +540,6 @@
     chips = devices // CORES
     columns = width // levels
     chunks = table.shape[0] // (CORES * LANES)
-    stages = frames // LANES
     tiles = frames // (2 * LANES)
     vmem = pl.BlockSpec(memory_space=pltpu.VMEM)
     anywhere = pl.BlockSpec(memory_space=pl.ANY)
@@ -504,8 +561,10 @@
             pltpu.VMEM((4, width, width), bf16),
             pltpu.VMEM((frames, width), f32),
             pltpu.VMEM((frames, columns), bf16),
-            pltpu.VMEM((columns // LANES, LANES + 16, frames), bf16),
+            pltpu.VMEM((columns // (width // HEADS), width // HEADS + 16, frames), bf16),
             pltpu.VMEM((frames, columns), bf16),
+            pltpu.VMEM((2 * LANES, width), bf16),
+            pltpu.VMEM((2 * LANES, width), bf16),
             pltpu.VMEM((frames, width), bf16),
             pltpu.VMEM((frames + 2 * PAD, width), bf16),
             pltpu.VMEM((frames, width), bf16),
@@ -514,16 +573,33 @@
             pltpu.VMEM((8, 2 * LANES), f32),
             pltpu.VMEM((8, 2 * LANES), f32),
             dma((11,)),
-            dma((4, levels)), dma((4, levels)), dma((2, levels, chunks)), dma((2, levels, chunks)),
-            dma((stages, levels)), dma((stages, levels)), dma((tiles,)),
+            dma((4, levels)), dma((4, levels)), dma((2, levels)), dma((2, levels, chunks)),
+            dma((levels,)), dma((tiles, levels)), dma((1,)),
         ]
         + [
-            dma((count, 2, half + extra)) for count in (3, 4) for extra in (0, 0, 1, 1)
+            dma(shape) for count in (3, 4) for shape in ((count,), (count, 2, half), (count,), (count,))
         ],
         compiler_params=pltpu.CompilerParams(
             collective_id=0, has_side_effects=True, vmem_limit_bytes=64000 * 1024
         ),
     )(tokens, decoded, done, fill, table, w_qkv, w_out_t, w_expand, w_project, taps)
+
+
+def head_kernel(final_ref, head_ref, logits_ref):
+    logits_ref[...] = dot_f32(final_ref[...], head_ref[...]).astype(logits_ref.dtype)
+
+
+def score(final, head):
+    frames, width = final.shape
+    codes = head.shape[1]
+    tile = 2 * LANES
+    return pl.pallas_call(
+        head_kernel,
+        out_shape=jax.ShapeDtypeStruct((frames, codes), final.dtype),
+        grid=(frames // tile,),
+        in_specs=[pl.BlockSpec((tile, width), lambda step: (step, 0)), pl.BlockSpec((width, codes), lambda step: (0, 0))],
+        out_specs=pl.BlockSpec((tile, codes), lambda step: (step, 0)),
+    )(final, head)
 
 
 def body(
@@ -543,7 +619,7 @@
         lax.axis_size("level"), lax.axis_size("dp"), token_ids[0], decoded_mask[0], levels_done, mask_vectors,
         code_tables[0], w_qkv, w_out.T, w_expand, w_project, w_depth,
     )
-    return dot_f32(final, level_heads[0]).astype(jnp.bfloat16)[None, None]
+    return score(final, level_heads[0])[None, None]
 
 
 def solution(mesh):

time: 109 us -> 97.6 us (0.90); the launches traced: 107 us -> 97.3 us
  matrix products: 7.65 us -> 0 us
  Pallas kernels: 99.1 us -> 96.6 us
    pallas_call x1, Pallas kernels: 99.1 us -> 88.6 us  [decode_step(): pl.pallas_call(functools.partial(step_kernel, levels, devices, frames, wi...]
    pallas_call x0 -> x1, Pallas kernels: none -> 8.01 us  [score(): pl.pallas_call(head_kernel, out_shape=jax.ShapeDtypeStruct((frames, codes...]
    dot_general x1 -> x0, matrix products: 7.65 us -> none  [dot_f32(): return jnp.dot(left, right, preferred_element_type=jnp.float32)]
where the time goes in v2:
time: 97.6 us; the launch traced here: 97.3 us
  Pallas kernels  96.6 us (99%)
    pallas_call x1, Pallas kernels, decode_step(): pl.pallas_call(functools.partial(step_kernel, levels, devices, frames, wi...  88.6 us
    pallas_call x1, Pallas kernels, score(): pl.pallas_call(head_kernel, out_shape=jax.ShapeDtypeStruct((frames, codes...  8.01 us

profile of v2, /device:TPU:0, one launch (start us, length us, event | category | flops | bytes accessed | tf_op | source)
XLA Modules:
  0.0 97.3 jit_solution(13221820686530253026)
XLA Ops:
  0.7 88.6 %shard_map.109.final_ref = bf16[1536,1024]{1,0:T(8,128)(2,1)} custom-call(s32[1,1536]{1,0:T(1,128)} %bitcast.9, s32[1,1536]{1,0:T(1,128)} %bitcast.10, s32[1]{0:T(128)S(6)} %copy.12.done_ref, bf16[1,1024]{1,0:T(2,128)(2,1)} %fill_ref.1, bf16[1024,1024]{1,0:T(8,128)(2,1)} %bitcast.6, bf16[3,64,512]{2,1,0:T(8,128)(2,1)} %qkv_ref.1, bf16[64,512]{1,0:T(8,128)(2,1)} %bitcast.8, ...), custom_call_target="tpu_custom_call" | custom-call | tf_op jit(solution)/shard_map/pallas_call | solution.py:549
  89.3 8.0 %shard_map.110 = bf16[1536,1024]{1,0:T(8,128)(2,1)} custom-call(bf16[1536,1024]{1,0:T(8,128)(2,1)} %shard_map.109.final_ref, bf16[1024,1024]{1,0:T(8,128)(2,1)} %bitcast.7), custom_call_target="tpu_custom_call" | custom-call | tf_op jit(solution)/shard_map/pallas_call | solution.py:596

commit v3 on v2

--- a/solution.py
+++ b/solution.py
@@ -240,7 +240,7 @@
     second = rings(rest, lambda part: rest_sources[part], 4, (ring_b, ring_b_recv, sib_b, sib_b_recv))
     hops = chips // 2
     turn = (1, 2, 0, 3)
-    slots = ("c1", "c2", "c3", "c3", "q0", "q1", "s0", "s1", "s2", "s2", "s3", "s4", "s4", "s5", "s5", "end")
+    slots = ("c1", "c2", "c3", "q0", "q0", "q1", "s0", "s1", "s2", "s2", "s3", "s4", "s4", "s5", "s5", "end")
     plan = {}
 
     def at_slot(slot, act):
@@ -285,8 +285,9 @@
     heads = columns // head_dim
     for head in range(heads):
         values_t[head, head_dim:, :] = jnp.ones((values_t.shape[1] - head_dim, frames), bf16)
+    groups = width // LANES
     for place in (pl.ds(0, PAD), pl.ds(PAD + frames, PAD)):
-        gated[place, :] = jnp.zeros((PAD, width), bf16)
+        gated[:, place, :] = jnp.zeros((groups, PAD, LANES), jnp.float32)
 
     for copy in early:
         copy.wait()
@@ -306,7 +307,7 @@
     lane = lax.broadcasted_iota(jnp.int32, (tile, LANES), 1).astype(jnp.float32)
 
     def span_of(step):
-        return pl.ds(pl.multiple_of(step * tile, tile), tile)
+        return pl.ds(step * tile if isinstance(step, int) else pl.multiple_of(step * tile, tile), tile)
 
     def onehot(found, start, count):
         return jnp.concatenate(
@@ -363,14 +364,19 @@
 
     scale = head_dim ** (-0.5)
 
-    def prepare(step, normed):
-        span = span_of(step)
-        total = embedded[span, :] + picked(last, levels - 1, span)
+    wide = 2 * tile
+    units = frames // wide
+
+    def prepare(unit, normed):
+        span = pl.ds(unit * wide, wide)
+        total = embedded[span, :] + jnp.concatenate(
+            [picked(last, levels - 1, span_of(2 * unit + half)) for half in range(2)], axis=0
+        )
         embedded[span, :] = total
         normed[...] = layer_norm(total).astype(bf16)
 
-    def project(step, normed):
-        span = span_of(step)
+    def project(unit, normed):
+        span = pl.ds(unit * wide, wide)
         queries[span, :] = dot_f32(normed[...], proj[0]).astype(bf16) * jnp.asarray(scale, bf16)
         keys[span, :] = dot_f32(normed[...], proj[1]).astype(bf16)
         found = dot_f32(normed[...], proj[2])
@@ -379,40 +385,39 @@
             values_t[2 * pair, 0:head_dim, span] = turned[0:head_dim]
             values_t[2 * pair + 1, 0:head_dim, span] = turned[head_dim:]
 
+    spare = (normed_a, normed_b)
     prepare(0, normed_a)
-
-    @pl.loop(0, tiles // 2)
-    def _(half):
-        for quarter in range(2):
-            @pl.when(half == min(1 + quarter, tiles // 2 - 1))
-            def _():
-                run(f"q{quarter}")
-
-        step = 2 * half
-        project(step, normed_a)
-        prepare(step + 1, normed_b)
-
-        project(step + 1, normed_b)
-
-        @pl.when(half < tiles // 2 - 1)
-        def _():
-            prepare(step + 2, normed_a)
-
-    def attended_copy(stage, shift, owner, target):
-        owner_columns = pl.ds(pl.multiple_of(owner * columns, columns), columns)
-        place = attended.at[span_of(stage), owner_columns]
+    for unit in range(units):
+        project(unit, spare[unit % 2])
+        if unit + 1 < units:
+            prepare(unit + 1, spare[(unit + 1) % 2])
+            if unit + 2 == units:
+                run("q1")
+            elif unit == 0:
+                run("q0")
+
+    pairs = heads // 2
+
+    def pieces_of(stage):
+        if isinstance(stage, int) and stage == 0:
+            return [(pair, pair * LANES, LANES) for pair in range(pairs)]
+        return [(stage + pairs - 1, 0, columns)]
+
+    def attended_copy(stage, piece, shift, owner, target):
+        index, start, count = piece
+        place = attended.at[span_of(stage), pl.ds(pl.multiple_of(owner * columns + start, LANES), count)]
         return pltpu.make_async_remote_copy(
             src_ref=place, dst_ref=place,
-            send_sem=att_send.at[shift], recv_sem=att_recv.at[stage, shift],
+            send_sem=att_send.at[shift], recv_sem=att_recv.at[index, shift],
             device_id={"level": target}, device_id_type=MESH,
         )
 
-    def attended_out(stage, shift):
-        return attended_copy(stage, shift, level, lax.rem(level + shift, levels))
-
-    def attended_in(stage, shift):
+    def attended_out(stage, piece, shift):
+        return attended_copy(stage, piece, shift, level, lax.rem(level + shift, levels))
+
+    def attended_in(stage, piece, shift):
         sender = lax.rem(level + levels - shift, levels)
-        return attended_copy(stage, shift, sender, sender)
+        return attended_copy(stage, piece, shift, sender, sender)
 
     lower = lax.broadcasted_iota(jnp.int32, (tile, LANES), 1) < head_dim
     part = frames // 2
@@ -445,18 +450,8 @@
 
     peaks_a[...] = score_part(masked_query(0, 0), 0, buffers[0], 0, frames)
 
-    @pl.loop(0, tiles)
-    def _(stage):
-        for sixth in range(6):
-            @pl.when(stage == sixth * tiles // 6)
-            def _():
-                run(f"s{sixth}")
-
-        @pl.when(stage > 0)
-        def _():
-            for shift in range(1, levels):
-                attended_out(stage - 1, shift).start()
-
+    def attend_all(stage):
+        pieces = pieces_of(stage)
         low = None
         for head in range(heads):
             ahead = (stage, head + 1) if head + 1 < heads else (lax.min(stage + 1, tiles - 1), 0)
@@ -466,25 +461,42 @@
             else:
                 across = pl.ds(pl.multiple_of(level * columns + head // 2 * LANES, LANES), LANES)
                 attended[span_of(stage), across] = jnp.concatenate([low, found], axis=0).T.astype(bf16)
-
-    for shift in range(1, levels):
-        attended_out(tiles - 1, shift).start()
+                if (head + 1) * len(pieces) % heads == 0:
+                    for shift in range(1, levels):
+                        attended_out(stage, pieces[(head + 1) * len(pieces) // heads - 1], shift).start()
+
+    run("s0")
+    attend_all(0)
+
+    @pl.loop(1, tiles)
+    def _(stage):
+        for sixth in range(1, 6):
+            @pl.when(stage == sixth * tiles // 6)
+            def _():
+                run(f"s{sixth}")
+
+        attend_all(stage)
+
     run("end")
-    for ring in second:
-        ring.finish()
+    for part in turn[:-1]:
+        second[part].finish()
 
     taps = depth_ref.shape[0]
     depth = depth_ref[...].astype(jnp.float32)
 
-    def gate(step):
-        for shift in range(1, levels):
-            attended_in(step, shift).wait_recv()
-        span = span_of(step)
+    def gate(step, count):
+        for ahead in range(count):
+            for piece in pieces_of(step + ahead):
+                for shift in range(1, levels):
+                    attended_in(step + ahead, piece, shift).wait_recv()
+        span = pl.ds(step * tile, count * tile)
         after_attn = embedded[span, :] + dot_nt(attended[span, :], rest[0])
         embedded[span, :] = after_attn
         normed = layer_norm(after_attn).astype(bf16)
         mixed = dot_f32(normed, rest[1]) * jax.nn.sigmoid(dot_f32(normed, rest[2]))
-        gated[pl.ds(pl.multiple_of(PAD + step * tile, PAD), tile), :] = mixed.astype(bf16)
+        mixed = mixed.astype(bf16).astype(jnp.float32)
+        for group in range(groups):
+            gated[group, pl.ds(PAD + step * tile, count * tile), :] = mixed[:, group * LANES : (group + 1) * LANES]
 
     def final_copy(step):
         span = span_of(step)
@@ -492,27 +504,32 @@
 
     def convolve(step):
         span = span_of(step)
-        start = pl.multiple_of(step * tile, tile)
-        window = gated[pl.ds(start, tile + 2 * PAD), :].astype(jnp.float32)
-        conv = jnp.zeros((tile, width), jnp.float32)
-        for tap in range(taps):
-            first_row = PAD - taps // 2 + tap
-            conv = conv + window[first_row : first_row + tile] * depth[tap : tap + 1, :]
+        conv = []
+        for group in range(groups):
+            across = slice(group * LANES, (group + 1) * LANES)
+            terms = [
+                gated[group, pl.ds(step * tile + (PAD - taps // 2 + tap), tile), :] * depth[tap : tap + 1, across]
+                for tap in range(taps)
+            ]
+            conv.append(functools.reduce(jnp.add, terms))
+        conv = jnp.concatenate(conv, axis=1)
         activated = (conv * jax.nn.sigmoid(conv)).astype(bf16)
         after_conv = embedded[span, :] + dot_f32(activated, rest[3])
         final[span, :] = layer_norm(after_conv).astype(bf16)
         final_copy(step).start()
 
-    gate(0)
-    gate(1)
-
-    @pl.loop(0, tiles - 2)
-    def _(step):
-        convolve(step)
-        gate(step + 2)
-
-    convolve(tiles - 2)
-    convolve(tiles - 1)
+    ready = convolved = 0
+    while convolved < tiles:
+        if ready < tiles:
+            count = 2 if ready + 4 <= tiles else 1
+            gate(ready, count)
+            if ready == 0:
+                second[turn[-1]].finish()
+            ready += count
+        limit = tiles if ready == tiles else ready - 1
+        while convolved < limit:
+            convolve(convolved)
+            convolved += 1
 
     for shift in range(1, levels):
         for kind in range(4):
@@ -563,10 +580,10 @@
             pltpu.VMEM((frames, columns), bf16),
             pltpu.VMEM((columns // (width // HEADS), width // HEADS + 16, frames), bf16),
             pltpu.VMEM((frames, columns), bf16),
-            pltpu.VMEM((2 * LANES, width), bf16),
-            pltpu.VMEM((2 * LANES, width), bf16),
+            pltpu.VMEM((4 * LANES, width), bf16),
+            pltpu.VMEM((4 * LANES, width), bf16),
             pltpu.VMEM((frames, width), bf16),
-            pltpu.VMEM((frames + 2 * PAD, width), bf16),
+            pltpu.VMEM((width // LANES, frames + 2 * PAD, LANES), f32),
             pltpu.VMEM((frames, width), bf16),
             pltpu.VMEM((frames, 2 * LANES), f32),
             pltpu.VMEM((frames, 2 * LANES), f32),
@@ -574,7 +591,7 @@
             pltpu.VMEM((8, 2 * LANES), f32),
             dma((11,)),
             dma((4, levels)), dma((4, levels)), dma((2, levels)), dma((2, levels, chunks)),
-            dma((levels,)), dma((tiles, levels)), dma((1,)),
+            dma((levels,)), dma((tiles + columns // LANES - 1, levels)), dma((1,)),
         ]
         + [
             dma(shape) for count in (3, 4) for shape in ((count,), (count, 2, half), (count,), (count,))
@@ -585,20 +602,40 @@
     )(tokens, decoded, done, fill, table, w_qkv, w_out_t, w_expand, w_project, taps)
 
 
-def head_kernel(final_ref, head_ref, logits_ref):
-    logits_ref[...] = dot_f32(final_ref[...], head_ref[...]).astype(logits_ref.dtype)
+def head_kernel(parts, final_ref, head_ref, logits_ref, final, head, logits, final_sem, head_sem, logits_sem):
+    rows, columns = final.shape[0] // parts, head.shape[1] // 2
+    spans = [pl.ds(part * rows, rows) for part in range(parts)]
+    sides = [pl.ds(side * columns, columns) for side in range(2)]
+    finals = [pltpu.make_async_copy(final_ref.at[span], final.at[span], final_sem.at[i]) for i, span in enumerate(spans)]
+    heads = [pltpu.make_async_copy(head_ref.at[:, side], head.at[:, side], head_sem.at[i]) for i, side in enumerate(sides)]
+    outs = [pltpu.make_async_copy(logits.at[span], logits_ref.at[span], logits_sem.at[i]) for i, span in enumerate(spans)]
+    for copy in finals[:1] + heads + finals[1:]:
+        copy.start()
+    for part, span in enumerate(spans):
+        finals[part].wait()
+        for which, side in enumerate(sides):
+            if part == 0:
+                heads[which].wait()
+            logits[span, side] = dot_f32(final[span, :], head[:, side]).astype(logits.dtype)
+        outs[part].start()
+    for copy in outs:
+        copy.wait()
 
 
 def score(final, head):
-    frames, width = final.shape
-    codes = head.shape[1]
-    tile = 2 * LANES
+    frames, codes = final.shape[0], head.shape[1]
+    parts = 3
+    hbm = pl.BlockSpec(memory_space=pltpu.HBM)
+    dma = pltpu.SemaphoreType.DMA
     return pl.pallas_call(
-        head_kernel,
+        functools.partial(head_kernel, parts),
         out_shape=jax.ShapeDtypeStruct((frames, codes), final.dtype),
-        grid=(frames // tile,),
-        in_specs=[pl.BlockSpec((tile, width), lambda step: (step, 0)), pl.BlockSpec((width, codes), lambda step: (0, 0))],
-        out_specs=pl.BlockSpec((tile, codes), lambda step: (step, 0)),
+        in_specs=[hbm, hbm],
+        out_specs=hbm,
+        scratch_shapes=[
+            pltpu.VMEM(final.shape, final.dtype), pltpu.VMEM(head.shape, head.dtype),
+            pltpu.VMEM((frames, codes), final.dtype), dma((parts,)), dma((2,)), dma((parts,)),
+        ],
     )(final, head)
 
 

time: 97.6 us -> 91.5 us (0.938)
  Pallas kernels: 96.6 us -> 90.5 us
    pallas_call x1, Pallas kernels: 88.6 us -> 84 us  [decode_step(): pl.pallas_call(functools.partial(step_kernel, levels, devices, frames, wi...]
    pallas_call x1, Pallas kernels: 8.01 us -> 6.51 us  [score(): pl.pallas_call(functools.partial(head_kernel, parts), out_shape=jax.Shape...]
where the time goes in v3:
time: 91.5 us; the launch traced here: 91.3 us
  Pallas kernels  90.5 us (99%)
    pallas_call x1, Pallas kernels, decode_step(): pl.pallas_call(functools.partial(step_kernel, levels, devices, frames, wi...  84 us
    pallas_call x1, Pallas kernels, score(): pl.pallas_call(functools.partial(head_kernel, parts), out_shape=jax.Shape...  6.51 us

profile of v3, /device:TPU:0, one launch (start us, length us, event | category | flops | bytes accessed | tf_op | source)
XLA Modules:
  0.0 91.3 jit_solution(16758492669881596536)
XLA Ops:
  0.7 84.0 %shard_map.109.final_ref = bf16[1536,1024]{1,0:T(8,128)(2,1)} custom-call(s32[1,1536]{1,0:T(1,128)} %bitcast.9, s32[1,1536]{1,0:T(1,128)} %bitcast.10, s32[1]{0:T(128)S(6)} %copy.12.done_ref, bf16[1,1024]{1,0:T(2,128)(2,1)} %fill_ref.1, bf16[1024,1024]{1,0:T(8,128)(2,1)} %bitcast.6, bf16[3,64,512]{2,1,0:T(8,128)(2,1)} %qkv_ref.1, bf16[64,512]{1,0:T(8,128)(2,1)} %bitcast.8, ...), custom_call_target="tpu_custom_call" | custom-call | tf_op jit(solution)/shard_map/pallas_call | solution.py:566
  84.6 6.5 %shard_map.110 = bf16[1536,1024]{1,0:T(8,128)(2,1)} custom-call(bf16[1536,1024]{1,0:T(8,128)(2,1)} %shard_map.109.final_ref, bf16[1024,1024]{1,0:T(8,128)(2,1)} %bitcast.7), custom_call_target="tpu_custom_call" | custom-call | tf_op jit(solution)/shard_map/pallas_call | solution.py:630

commit v4 on v3

--- a/solution.py
+++ b/solution.py
@@ -240,7 +240,7 @@
     second = rings(rest, lambda part: rest_sources[part], 4, (ring_b, ring_b_recv, sib_b, sib_b_recv))
     hops = chips // 2
     turn = (1, 2, 0, 3)
-    slots = ("c1", "c2", "c3", "q0", "q0", "q1", "s0", "s1", "s2", "s2", "s3", "s4", "s4", "s5", "s5", "end")
+    slots = ("c1", "c2", "c3", "q0", "q0", "q1", "s0", "s1", "s2", "s3", "s3", "s4", "s5", "s5", "end", "end")
     plan = {}
 
     def at_slot(slot, act):

time: 91.5 us -> 91.5 us (level)
  no operation moved by 1% of the time
where the time goes in v4:
time: 91.5 us; the launch traced here: 91.3 us
  Pallas kernels  90.4 us (99%)
    pallas_call x1, Pallas kernels, decode_step(): pl.pallas_call(functools.partial(step_kernel, levels, devices, frames, wi...  83.9 us
    pallas_call x1, Pallas kernels, score(): pl.pallas_call(functools.partial(head_kernel, parts), out_shape=jax.Shape...  6.51 us

profile of v4, /device:TPU:0, one launch (start us, length us, event | category | flops | bytes accessed | tf_op | source)
XLA Modules:
  0.0 91.3 jit_solution(11691432280784547166)
XLA Ops:
  0.7 83.9 %shard_map.109.final_ref = bf16[1536,1024]{1,0:T(8,128)(2,1)} custom-call(s32[1,1536]{1,0:T(1,128)} %bitcast.9, s32[1,1536]{1,0:T(1,128)} %bitcast.10, s32[1]{0:T(128)S(6)} %copy.12.done_ref, bf16[1,1024]{1,0:T(2,128)(2,1)} %fill_ref.1, bf16[1024,1024]{1,0:T(8,128)(2,1)} %bitcast.6, bf16[3,64,512]{2,1,0:T(8,128)(2,1)} %qkv_ref.1, bf16[64,512]{1,0:T(8,128)(2,1)} %bitcast.8, ...), custom_call_target="tpu_custom_call" | custom-call | tf_op jit(solution)/shard_map/pallas_call | solution.py:566
  84.6 6.5 %shard_map.110 = bf16[1536,1024]{1,0:T(8,128)(2,1)} custom-call(bf16[1536,1024]{1,0:T(8,128)(2,1)} %shard_map.109.final_ref, bf16[1024,1024]{1,0:T(8,128)(2,1)} %bitcast.7), custom_call_target="tpu_custom_call" | custom-call | tf_op jit(solution)/shard_map/pallas_call | solution.py:630
